TPU v7x, 256 devices: a whole 4x4x8 slice. The times are simulated.
256 devices in a mesh: gx: 16 (over z, x_lo), gz: 16 (over y, x_hi, core).
Axes of the slice: x: 4 (x_hi: 2, x_lo: 2; x = x_hi * 2 + x_lo), y: 4, z: 8, core: 2. Of those that a mesh axis runs over, the one named last changes fastest.
Arguments:
- velocity: float32 [3, 128, 512, 384], P(None, 'gx', 'gz'), may hold values from -6 to 6
- y_gap: float32 [385], replicated, may hold values from 0.2 to 2
Outputs:
- eddy_visc: float32 [128, 512, 384], P('gx', 'gz')
- lm_field: float32 [128, 512, 384], P('gx', 'gz')
- mm_field: float32 [128, 512, 384], P('gx', 'gz')
- coefficient: float32 [384], replicated
All inputs are finite; a program needn't handle non-finite values.
Results may differ from a plain program's by a relative error of at most 0.00002.
Values sent between devices are 32-bit elements; how exact they have to be, the bound alone decides.
No kernel may reach another device: no remote copies, remote signals or barrier semaphores. Data moves between devices by JAX's collectives and lax.ppermute only.
A program may use at most 64 MiB of HBM per device.

v0:
```python
import functools

import jax
import jax.numpy as jnp
from jax import lax
from jax.experimental import pallas as pl
from jax.experimental.pallas import tpu as pltpu
from jax.sharding import Mesh
from jax.sharding import PartitionSpec as P


GX = ("gx_0", "gx_1")
GZ = ("gz_0", "gz_1", "gz_2")

LANES = 128
SUB = 8
TOP = 8
HALO = 2
QUAD = 2 * HALO
EARLY = 16


def exchange(last, leading, axis):
    size = lax.axis_size(axis)
    up = [(i, (i + 1) % size) for i in range(size)]
    down = [(j, i) for i, j in up]
    before = lax.ppermute(last, axis, up)
    after = lax.ppermute(leading, axis, down)
    return before, after


def over_axes(copies):
    half = jnp.sum(lax.all_to_all(copies, ("gx_0", "gz_2"), 0, 0, tiled=True), axis=0)
    copies = jnp.broadcast_to(half[None], copies.shape)
    return lax.all_to_all(copies, ("gx_1", "gz_0", "gz_1"), 0, 0, tiled=True)


def width_square(y_gap):
    return (0.5 * (y_gap[:-1] + y_gap[1:])) ** (2.0 / 3.0)


def strain_of(ref, slopes, at, chunk, row):
    def cell(k, step_x=0, step_z=0):
        return ref[k, at + step_x, chunk, pl.ds(row + step_z, SUB), :]

    along_x = [cell(k, 1) - cell(k, -1) for k in range(3)]
    along_z = [cell(k, 0, 1) - cell(k, 0, -1) for k in range(3)]
    parts = [
        along_x[0],
        slopes[1],
        along_z[2],
        slopes[0] + along_x[1],
        along_z[0] + along_x[2],
        along_z[1] + slopes[2],
    ]
    squares = [part * part for part in parts]
    square = 0.5 * (squares[0] + squares[1] + squares[2]) + 0.25 * (
        squares[3] + squares[4] + squares[5]
    )
    return parts, jnp.sqrt(square)


def wall_slopes(read, inverse, chunks):
    lane = lax.broadcasted_iota(jnp.int32, (SUB, LANES), 1)
    values = [read(c) for c in range(chunks)]
    ahead = [pltpu.roll(value, LANES - 1, 1) for value in values] + [jnp.zeros_like(values[0])]
    behind = [jnp.zeros_like(values[0])] + [pltpu.roll(value, 1, 1) for value in values]
    return [
        (
            jnp.where(lane == LANES - 1, ahead[c + 1], ahead[c])
            - jnp.where(lane == 0, behind[c], behind[c + 1])
        )
        * inverse[c]
        for c in range(chunks)
    ]


PAIRS = ((0, 0), (1, 1), (2, 2), (0, 1), (0, 2), (1, 2))


def smooth(below, here, above):
    return (below + above) + (here + here)


def column(c):
    return slice(c * LANES, (c + 1) * LANES)


def put_layer(cells, at, rows, value):
    for k in range(3):
        for c in range(value(k).shape[-1] // LANES):
            cells[k, at, c, rows, :] = value(k)[:, column(c)]


def split_kernel(v_ref, first_early, last_early, first_late, last_late, first_z, last_z, cells):
    _, nx, nz, _ = v_ref.shape
    early = first_early.shape[2]
    for k in range(3):
        for j in range(HALO):
            for at, head, tail in ((j, first_early, first_late), (nx - HALO + j, last_early, last_late)):
                head[k, j] = v_ref[k, at, :early, :]
                for q in range(tail.shape[2]):
                    row = early + QUAD * q
                    tail[k, j, q] = v_ref[k, at, row : row + QUAD, :]
        for i in range(nx):
            first_z[k, i] = v_ref[k, i, :HALO, :]
            last_z[k, i] = v_ref[k, i, nz - HALO :, :]

    def own(i, carry):
        put_layer(cells, i + HALO, slice(TOP, TOP + nz), lambda k: v_ref[k, i])
        return carry

    lax.fori_loop(0, nx, own, 0)


def layer_pass(i, inverse, cells, filtered, smoothed, size_ref, sizes, products):
    chunks, nz = filtered.shape[2:4]
    nx = cells.shape[1] - 2 * HALO
    blocks = nz // SUB
    wide = [TOP - 1 + SUB * b for b in range(blocks + 1)]
    at = i + 1
    for row in wide:
        per_speed = [
            wall_slopes(lambda c: cells[k, at, c, pl.ds(row, SUB), :], inverse, chunks)
            for k in range(3)
        ]
        for c in range(chunks):
            parts, size = strain_of(cells, [per_speed[k][c] for k in range(3)], at, c, row)
            sizes[c, pl.ds(row, SUB), :] = size
            speeds = [cells[k, at, c, pl.ds(row, SUB), :] for k in range(3)]
            for n in range(6):
                products[n, c, pl.ds(row, SUB), :] = size * parts[n]
                p, q = PAIRS[n]
                products[6 + n, c, pl.ds(row, SUB), :] = speeds[p] * speeds[q]
    for c in range(chunks):
        for b in range(blocks):
            row = TOP + SUB * b
            for n in range(12):
                filtered[n, i, c, pl.ds(SUB * b, SUB), :] = smooth(
                    *[products[n, c, pl.ds(row + s, SUB), :] for s in (-1, 0, 1)]
                )

    @pl.when(jnp.logical_and(i >= 1, i <= nx))
    def _():
        for c in range(chunks):
            for b in range(blocks):
                size_ref[i - 1, SUB * b : SUB * (b + 1), column(c)] = sizes[
                    c, TOP + SUB * b : TOP + SUB * (b + 1), :
                ]

    for k in range(3):
        for c in range(chunks):
            for b in range(blocks + 2):
                row = SUB * b
                products[k, c, pl.ds(row, SUB), :] = smooth(
                    *[cells[k, at + s, c, pl.ds(row, SUB), :] for s in (-1, 0, 1)]
                )
            for row in wide:
                smoothed[k, i, c, pl.ds(row, SUB), :] = smooth(
                    *[products[k, c, pl.ds(row + s, SUB), :] for s in (-1, 0, 1)]
                )


def result_pass(i, inverse, width, filtered, smoothed, lm_ref, mm_ref, totals):
    chunks, nz = filtered.shape[2:4]
    at = i + 1
    add = functools.partial(functools.reduce, jnp.add)
    for b in range(nz // SUB):
        row = TOP + SUB * b
        per_speed = [
            wall_slopes(lambda c: smoothed[k, at, c, pl.ds(row, SUB), :], inverse, chunks)
            for k in range(3)
        ]
        for c in range(chunks):
            parts, size = strain_of(smoothed, [per_speed[k][c] for k in range(3)], at, c, row)
            size = 0.25 * size
            speeds = [0.25 * smoothed[k, at, c, pl.ds(row, SUB), :] for k in range(3)]

            def over_x(n):
                return smooth(*[filtered[n, i + s, c, pl.ds(SUB * b, SUB), :] for s in range(3)])

            cross, diagonal, outside = [], [], []
            for n in range(6):
                model = over_x(n) - size * parts[n]
                p, q = PAIRS[n]
                cross.append((over_x(6 + n) - speeds[p] * speeds[q]) * model)
                (diagonal if n < 3 else outside).append(model * model)
            lm = (width[c] * (1.0 / 256.0)) * add(cross)
            mm = (width[c] * width[c] * (1.0 / 256.0)) * (add(diagonal) + 0.5 * add(outside))
            lm_ref[i, SUB * b : SUB * (b + 1), column(c)] = lm
            mm_ref[i, SUB * b : SUB * (b + 1), column(c)] = mm
            totals[0, c] += lm
            totals[1, c] += mm


def rows_of(ref):
    return [
        jnp.broadcast_to(ref[:, column(c)], (SUB, LANES)) for c in range(ref.shape[-1] // LANES)
    ]


def inner_kernel(
    before_z, after_z, inv_ref, width_ref, cells_in,
    cells, filtered, smoothed, lm_ref, mm_ref, size_ref, totals,
    sizes, products,
):
    nx, nz, _ = lm_ref.shape

    def sides(i, carry):
        put_layer(cells, i + HALO, slice(TOP - HALO, TOP), lambda k: before_z[k, i])
        put_layer(cells, i + HALO, slice(TOP + nz, TOP + nz + HALO), lambda k: after_z[k, i])
        return carry

    lax.fori_loop(0, nx, sides, 0)
    inverse, width = rows_of(inv_ref), rows_of(width_ref)

    def layer(i, carry):
        layer_pass(i, inverse, cells, filtered, smoothed, size_ref, sizes, products)
        return carry

    lax.fori_loop(HALO, nx, layer, 0)
    totals[...] = jnp.zeros_like(totals)

    def result(i, carry):
        result_pass(i, inverse, width, filtered, smoothed, lm_ref, mm_ref, totals)
        return carry

    lax.fori_loop(HALO, nx - HALO, result, 0)


def outer_kernel(
    before_early, after_early, before_late, after_late, inv_ref, width_ref,
    cells_in, filtered_in, smoothed_in, lm_in, mm_in, size_in, totals_in,
    cells, filtered, smoothed, lm_ref, mm_ref, size_ref, totals, copies,
    sizes, products,
):
    nx, nz, _ = lm_ref.shape
    for j in range(HALO):
        for at, head, tail in ((j, before_early, before_late), (nx + HALO + j, after_early, after_late)):
            early, quads = head.shape[2], tail.shape[2] - 1
            put_layer(cells, at, slice(TOP, TOP + early), lambda k: head[k, j])
            for q in range(quads):
                row = TOP + early + QUAD * q
                put_layer(cells, at, slice(row, row + QUAD), lambda k: tail[k, j, q])
            put_layer(cells, at, slice(TOP - HALO, TOP), lambda k: tail[k, j, quads, :HALO, :])
            put_layer(cells, at, slice(TOP + nz, TOP + nz + HALO), lambda k: tail[k, j, quads, HALO:, :])
    inverse, width = rows_of(inv_ref), rows_of(width_ref)

    def layer(j, carry):
        i = jnp.where(j < HALO, j, j + nx - HALO)
        layer_pass(i, inverse, cells, filtered, smoothed, size_ref, sizes, products)
        return carry

    lax.fori_loop(0, 2 * HALO, layer, 0)

    def result(j, carry):
        i = jnp.where(j < HALO, j, j + nx - 2 * HALO)
        result_pass(i, inverse, width, filtered, smoothed, lm_ref, mm_ref, totals)
        return carry

    lax.fori_loop(0, 2 * HALO, result, 0)
    for n in range(2):
        for c in range(totals.shape[1]):
            line = jnp.sum(totals[n, c], axis=0, keepdims=True)
            for member in range(copies.shape[0]):
                copies[member, n : n + 1, column(c)] = line


def finish_kernel(
    planes, parts_ref, width_ref, lm_ref, mm_ref, size_ref,
    eddy_out, lm_out, mm_out, coefficient_ref,
    eddy_ref, sems,
):
    stores = [
        pltpu.make_async_copy(lm_ref, lm_out, sems.at[0]),
        pltpu.make_async_copy(mm_ref, mm_out, sems.at[1]),
        pltpu.make_async_copy(eddy_ref, eddy_out, sems.at[2]),
    ]
    stores[0].start()
    stores[1].start()
    total = parts_ref[0]
    for member in range(1, parts_ref.shape[0]):
        total = total + parts_ref[member]
    coefficient = total[0:1] / planes / (total[1:2] / planes + 1e-06)
    coefficient_ref[...] = coefficient[0]
    eddy_ref[...] = (coefficient * width_ref[...])[None] * size_ref[...]
    stores[2].start()
    for store in stores:
        store.wait()


def call(kernel, outs, scratch, flops, aliases, args):
    whole = pl.BlockSpec(memory_space=pltpu.VMEM)
    return pl.pallas_call(
        kernel,
        out_shape=tuple(pltpu.VMEM(shape, jnp.float32) for shape in outs),
        in_specs=[whole] * len(args),
        out_specs=tuple([whole] * len(outs)),
        scratch_shapes=scratch,
        input_output_aliases=aliases,
        cost_estimate=pl.CostEstimate(flops=flops, bytes_accessed=0, transcendentals=0),
        compiler_params=pltpu.CompilerParams(vmem_limit_bytes=VMEM_LIMIT),
    )(*args)


VMEM_LIMIT = 16 * 2**20


def per_device(velocity, y_gap):
    _, nx, nz, ny = velocity.shape
    chunks, rows = ny // LANES, nz + 2 * SUB
    width_sq = width_square(y_gap)
    inverse = 2.0 / (y_gap[:-1] + y_gap[1:])
    lines = (inverse[None], width_sq[None])

    cells_shape = (3, nx + 2 * HALO, chunks, rows, LANES)
    field = (nx, nz, ny)
    quads = (nz - EARLY) // QUAD
    first_early, last_early, first_late, last_late, first_z, last_z, cells = call(
        split_kernel,
        [(3, HALO, EARLY, ny)] * 2 + [(3, HALO, quads, QUAD, ny)] * 2 + [(3, nx, HALO, ny)] * 2
        + [cells_shape],
        [], 0, {}, (velocity,),
    )
    before_z, after_z = exchange(last_z, first_z, GZ)
    before_early, after_early = exchange(last_early, first_early, GX)
    near = jnp.concatenate([before_z, after_z], axis=2)[:, :, None]
    before_late, after_late = exchange(
        jnp.concatenate([last_late, near[:, nx - HALO :]], axis=2),
        jnp.concatenate([first_late, near[:, :HALO]], axis=2),
        GX,
    )

    scratch = [
        pltpu.VMEM((chunks, rows, LANES), jnp.float32),
        pltpu.VMEM((12, chunks, rows, LANES), jnp.float32),
    ]
    state_shapes = [
        cells_shape,
        (12, nx + 2, chunks, nz, LANES),
        (3, nx + 2, chunks, rows, LANES),
        field, field, field,
        (2, chunks, SUB, LANES),
    ]
    state = call(
        inner_kernel, state_shapes, scratch, 20_000_000, {4: 0},
        (before_z, after_z, *lines, cells),
    )
    *state, copies = call(
        outer_kernel, [*state_shapes, (16, 2, ny)], scratch, 20_000_000,
        {6 + n: n for n in range(7)},
        (before_early, after_early, before_late, after_late, *lines, *state),
    )
    lm_field, mm_field, strain_size = state[3:6]
    planes = nx * lax.axis_size(GX) * nz * lax.axis_size(GZ)
    whole, there = pl.BlockSpec(memory_space=pltpu.VMEM), pl.BlockSpec(memory_space=pl.ANY)
    block = jax.ShapeDtypeStruct(field, jnp.float32)
    eddy_visc, lm_field, mm_field, coefficient = pl.pallas_call(
        functools.partial(finish_kernel, planes),
        out_shape=(block, block, block, jax.ShapeDtypeStruct((ny,), jnp.float32)),
        in_specs=[whole] * 5,
        out_specs=(there, there, there, whole),
        scratch_shapes=[pltpu.VMEM(field, jnp.float32), pltpu.SemaphoreType.DMA((3,))],
        name="finish",
        compiler_params=pltpu.CompilerParams(vmem_limit_bytes=VMEM_LIMIT),
    )(over_axes(copies), lines[1], lm_field, mm_field, strain_size)
    return (eddy_visc, lm_field, mm_field, coefficient)


def solution(mesh):
    torus = Mesh(mesh.devices.reshape(8, 2, 4, 2, 2), ("gx_0", "gx_1", "gz_0", "gz_1", "gz_2"))

    return jax.shard_map(
        per_device,
        mesh=torus,
        in_specs=(P(None, GX, GZ, None), P()),
        out_specs=(P(GX, GZ, None), P(GX, GZ, None), P(GX, GZ, None), P()),
        check_vma=False,
    )
```

profile of v0, /device:TPU:1, one launch (start us, length us, event | category | flops | bytes accessed | tf_op | source)
XLA Modules:
  0.0 57.5 jit_solution(10051754426342282862)
XLA Ops:
  0.6 0.0 copy-start
  0.6 1.3 %copy-done = f32[3,8,32,384]{3,2,1,0:T(8,128)S(1)} copy-done((f32[3,8,32,384]{3,2,1,0:T(8,128)S(1)}, f32[3,8,32,384]{3,2,1,0:T(8,128)}, u32[]{:S(2)}) %copy-start) | copy-done | bytes 1179672
  1.9 0.2 shard_map.57
  2.1 4.2 %collective-permute-start.2 = (f32[3,8,2,384]{3,2,1,0:T(2,128)S(1)}, f32[3,8,2,384]{3,2,1,0:T(2,128)S(1)}, u32[]{:S(2)}, u32[]{:S(2)}) collective-permute-start(f32[3,8,2,384]{3,2,1,0:T(2,128)S(1)} %get-tuple-element.25), channel_id=1, source_target_pairs={{0,1},{1,2},{2,3},{3,4},{4,5},{5,6},{6,7},{7,8},{8,9},{9,10},{10,1... | collective-permute-start | bytes 221192 | tf_op jit(solution)/shard_map/ppermute | solution.py:27
  6.3 0.0 collective-permute-start.3
  6.3 0.3 collective-permute-start
  6.6 5.3 %collective-permute-start.1 = (f32[3,2,16,384]{3,2,1,0:T(8,128)S(1)}, f32[3,2,16,384]{3,2,1,0:T(8,128)S(1)}, u32[]{:S(2)}, u32[]{:S(2)}) collective-permute-start(f32[3,2,16,384]{3,2,1,0:T(8,128)S(1)} %get-tuple-element.23), channel_id=1, source_target_pairs={{16,0},{32,16},{48,32},{64,48},{80,64},{96,80},{112,96},{128,112},... | collective-permute-start | bytes 442376 | tf_op jit(solution)/shard_map/ppermute | solution.py:28
  11.9 0.0 collective-permute-done.2.before_z
  11.9 2.0 %collective-permute-done.3.after_z = f32[3,8,2,384]{3,2,1,0:T(2,128)S(1)} collective-permute-done((f32[3,8,2,384]{3,2,1,0:T(2,128)S(1)}, f32[3,8,2,384]{3,2,1,0:T(2,128)S(1)}, u32[]{:S(2)}, u32[]{:S(2)}) %collective-permute-start.3) | collective-permute-done | bytes 73760 | tf_op jit(solution)/shard_map/ppermute | solution.py:28
  13.9 0.1 maximum_bitcast_fusion
  14.1 0.1 collective-permute-start.4
  14.2 6.5 %collective-permute-start.5 = (f32[3,2,5,4,384]{4,3,2,1,0:T(4,128)S(1)}, f32[3,2,5,4,384]{4,3,2,1,0:T(4,128)S(1)}, u32[]{:S(2)}, u32[]{:S(2)}) collective-permute-start(f32[3,2,5,4,384]{4,3,2,1,0:T(4,128)S(1)} %pad_maximum_fusion.1), channel_id=1, source_target_pairs={{16,0},{32,16},{48,32},{64,48},{80,64},{96,80},{112,96},{128,112},... | collective-permute-start | bytes 552968 | tf_op jit(solution)/shard_map/ppermute | solution.py:28
  20.7 0.8 %multiply_power_fusion = (f32[384]{0:T(512)S(1)}, f32[384]{0:T(512)S(1)}) fusion(f32[385]{0:T(512)} %param.3), kind=kLoop, calls=%fused_computation.3 | loop fusion | flops 1152 | bytes 6144 | tf_op jit(solution)/shard_map/pow | solution.py:39
  21.6 3.8 %shard_map.58 = (f32[3,12,3,48,128]{4,3,2,1,0:T(8,128)S(1)}, f32[12,10,3,32,128]{4,3,2,1,0:T(8,128)S(1)}, f32[3,10,3,48,128]{4,3,2,1,0:T(8,128)S(1)}, f32[8,32,3...) custom-call(f32[3,8,2,384]{3,2,1,0:T(2,128)S(1)} %collective-permute, ...), custom_call_target="tpu_custom_call", output_to_operand_aliasing={{0}: (4, {})} | custom-call | flops 20000000 | tf_op jit(solution)/shard_map/pallas_call | solution.py:294
  25.4 0.0 collective-permute-done.before_early
  25.4 0.0 collective-permute-done.1.after_early
  25.4 0.0 collective-permute-done.4.before_late
  25.5 0.1 collective-permute-done.5.after_late
  25.6 3.1 %shard_map.59 = (f32[3,12,3,48,128]{4,3,2,1,0:T(8,128)S(1)}, f32[12,10,3,32,128]{4,3,2,1,0:T(8,128)S(1)}, f32[3,10,3,48,128]{4,3,2,1,0:T(8,128)S(1)}, f32[8,32,3...) custom-call(f32[3,2,16,384]{3,2,1,0:T(8,128)S(1)} %collective-permut, ...), custom_call_target="tpu_custom_call", output_to_operand_aliasing={{0}: (6, {}), {1}: (7, {}), {2}: (8, {}), {3}: (9, {}), {4}... | custom-call | flops 20000000 | tf_op jit(solution)/shard_map/pallas_call | solution.py:294
  28.7 14.8 %all_to_all.10 = f32[16,2,384]{2,1,0:T(2,128)S(1)} all-to-all(f32[16,2,384]{2,1,0:T(2,128)S(1)} %get-tuple-element.36), channel_id=1, replica_groups=mesh['gx_0'=8,'gx_1'=2,'gz_0'=4,'gz_1'=2,'gz_2'=2] {'gx_0','gz_2'}, dimensions={0} | all-to-all | bytes 98304 | tf_op jit(solution)/shard_map/all_to_all | solution.py:33
  43.6 12.4 %all_to_all.11.parts_ref = f32[16,2,384]{2,1,0:T(2,128)S(1)} all-to-all(f32[16,2,384]{2,1,0:T(2,128)S(1)} %broadcast_in_dim.18), channel_id=1, replica_groups=mesh['gx_0'=8,'gx_1'=2,'gz_0'=4,'gz_1'=2,'gz_2'=2] {'gx_1','gz_0','gz_1'}, dimensions={0} | all-to-all | bytes 98304 | tf_op jit(solution)/shard_map/all_to_all | solution.py:35
  55.9 1.6 %finish.1 = (f32[8,32,384]{2,1,0:T(8,128)}, f32[8,32,384]{2,1,0:T(8,128)}, f32[8,32,384]{2,1,0:T(8,128)}, f32[384]{0:T(512)}) custom-call(f32[16,2,384]{2,1,0:T(2,128)S(1)} %all_to_all.11.parts_ref, f32[1,384]{1,0:T(1,128)S(1)} %broadcast_in_dim.17.width_ref, f32[8,32,384]{2,1,0:T(8,128)S(1)} %get-tuple-element.37.lm_ref, ...), custom_call_target="tpu_custom_call" | custom-call | tf_op jit(solution)/shard_map/finish/pallas_call | solution.py:358
  (7 shorter events, 0.2 us)
Async XLA Ops:
  0.6 1.3 %copy-start = (f32[3,8,32,384]{3,2,1,0:T(8,128)S(1)}, f32[3,8,32,384]{3,2,1,0:T(8,128)}, u32[]{:S(2)}) copy-start(f32[3,8,32,384]{3,2,1,0:T(8,128)} %v_ref.1) | copy-start | bytes 3538948
  2.1 9.8 %collective-permute-start.2 = (f32[3,8,2,384]{3,2,1,0:T(2,128)S(1)}, f32[3,8,2,384]{3,2,1,0:T(2,128)S(1)}, u32[]{:S(2)}, u32[]{:S(2)}) collective-permute-start(f32[3,8,2,384]{3,2,1,0:T(2,128)S(1)} %get-tuple-element.25), channel_id=1, source_target_pairs={{0,1},{1,2},{2,3},{3,4},{4,5},{5,6},{6,7},{7,8},{8,9},{9,10},{10,1... | collective-permute-start | bytes 221192 | tf_op jit(solution)/shard_map/ppermute | solution.py:27
  6.3 7.7 %collective-permute-start.3 = (f32[3,8,2,384]{3,2,1,0:T(2,128)S(1)}, f32[3,8,2,384]{3,2,1,0:T(2,128)S(1)}, u32[]{:S(2)}, u32[]{:S(2)}) collective-permute-start(f32[3,8,2,384]{3,2,1,0:T(2,128)S(1)} %get-tuple-element.26), channel_id=1, source_target_pairs={{1,0},{2,1},{3,2},{4,3},{5,4},{6,5},{7,6},{8,7},{9,8},{10,9},{11,1... | collective-permute-start | bytes 221192 | tf_op jit(solution)/shard_map/ppermute | solution.py:28
  6.3 19.1 %collective-permute-start = (f32[3,2,16,384]{3,2,1,0:T(8,128)S(1)}, f32[3,2,16,384]{3,2,1,0:T(8,128)S(1)}, u32[]{:S(2)}, u32[]{:S(2)}) collective-permute-start(f32[3,2,16,384]{3,2,1,0:T(8,128)S(1)} %get-tuple-element.22), channel_id=1, source_target_pairs={{0,16},{16,32},{32,48},{48,64},{64,80},{80,96},{96,112},{112,128},... | collective-permute-start | bytes 442376 | tf_op jit(solution)/shard_map/ppermute | solution.py:27
  6.6 18.8 %collective-permute-start.1 = (f32[3,2,16,384]{3,2,1,0:T(8,128)S(1)}, f32[3,2,16,384]{3,2,1,0:T(8,128)S(1)}, u32[]{:S(2)}, u32[]{:S(2)}) collective-permute-start(f32[3,2,16,384]{3,2,1,0:T(8,128)S(1)} %get-tuple-element.23), channel_id=1, source_target_pairs={{16,0},{32,16},{48,32},{64,48},{80,64},{96,80},{112,96},{128,112},... | collective-permute-start | bytes 442376 | tf_op jit(solution)/shard_map/ppermute | solution.py:28
  14.1 11.4 %collective-permute-start.4 = (f32[3,2,5,4,384]{4,3,2,1,0:T(4,128)S(1)}, f32[3,2,5,4,384]{4,3,2,1,0:T(4,128)S(1)}, u32[]{:S(2)}, u32[]{:S(2)}) collective-permute-start(f32[3,2,5,4,384]{4,3,2,1,0:T(4,128)S(1)} %pad_maximum_fusion), channel_id=1, source_target_pairs={{0,16},{16,32},{32,48},{48,64},{64,80},{80,96},{96,112},{112,128},... | collective-permute-start | bytes 552968 | tf_op jit(solution)/shard_map/ppermute | solution.py:27
  14.2 11.4 %collective-permute-start.5 = (f32[3,2,5,4,384]{4,3,2,1,0:T(4,128)S(1)}, f32[3,2,5,4,384]{4,3,2,1,0:T(4,128)S(1)}, u32[]{:S(2)}, u32[]{:S(2)}) collective-permute-start(f32[3,2,5,4,384]{4,3,2,1,0:T(4,128)S(1)} %pad_maximum_fusion.1), channel_id=1, source_target_pairs={{16,0},{32,16},{48,32},{64,48},{80,64},{96,80},{112,96},{128,112},... | collective-permute-start | bytes 552968 | tf_op jit(solution)/shard_map/ppermute | solution.py:28
where the time goes:
time: 57.7 us; the launch traced here: 57.5 us
  blocking collectives  27.2 us (47%)
  starting transfers between devices  16.4 us (28%)
  Pallas kernels  8.69 us (15%)
  waiting for transfers between devices  2.19 us (4%)
  local copies, waits for them, and re-layouts  1.3 us (2%)
  other arithmetic  1.04 us (2%)
  between operations  0.74 us (1%)
    all_to_all x1, blocking collectives, over_axes(): lax.all_to_all(copies, ('gx_0', 'gz_2'), 0, 0, tiled=True)  14.8 us
    all_to_all x1, blocking collectives, over_axes(): return lax.all_to_all(copies, ('gx_1', 'gz_0', 'gz_1'), 0, 0, tiled=True)  12.4 us
    ppermute x3, starting transfers between devices, exchange(): after = lax.ppermute(leading, axis, down)  11.8 us
    pallas_call x3, Pallas kernels, call(): pl.pallas_call(kernel, out_shape=tuple((pltpu.VMEM(shape, jnp.float32) fo...  7.1 us
    ppermute x3, starting transfers between devices, exchange(): before = lax.ppermute(last, axis, up)  4.59 us
    ppermute x3, waiting for transfers between devices, exchange(): after = lax.ppermute(leading, axis, down)  2.18 us
    pallas_call x1, Pallas kernels, per_device(): pl.pallas_call(functools.partial(finish_kernel, planes), out_shape=(block...  1.59 us
    unnamed x2, local copies, waits for them, and re-layouts  1.26 us
  transfers between devices with their start and end apart: 6, of which 2 were waited for; matrix products, arithmetic and copies ran while one was open for 2% of the time, Pallas kernels for 7%

commit v1 on v0

--- a/solution.py
+++ b/solution.py
@@ -16,23 +16,26 @@
 SUB = 8
 TOP = 8
 HALO = 2
+EARLY_UP, EARLY_DOWN = 16, 16
 QUAD = 2 * HALO
-EARLY = 16
-
-
-def exchange(last, leading, axis):
+
+
+def send(array, axis, step):
     size = lax.axis_size(axis)
-    up = [(i, (i + 1) % size) for i in range(size)]
-    down = [(j, i) for i, j in up]
-    before = lax.ppermute(last, axis, up)
-    after = lax.ppermute(leading, axis, down)
-    return before, after
+    return lax.ppermute(array, axis, [(i, (i + step) % size) for i in range(size)])
+
+
+GROUPS = (("gx_1", "gz_0", "gz_1", "gz_2"), ("gx_0",))
+
+
+def members(axes):
+    return functools.reduce(lambda count, axis: count * lax.axis_size(axis), axes, 1)
 
 
 def over_axes(copies):
-    half = jnp.sum(lax.all_to_all(copies, ("gx_0", "gz_2"), 0, 0, tiled=True), axis=0)
-    copies = jnp.broadcast_to(half[None], copies.shape)
-    return lax.all_to_all(copies, ("gx_1", "gz_0", "gz_1"), 0, 0, tiled=True)
+    half = jnp.sum(lax.all_to_all(copies, GROUPS[0], 0, 0, tiled=True), axis=0)
+    copies = jnp.broadcast_to(half[None], (members(GROUPS[1]), *half.shape))
+    return lax.all_to_all(copies, GROUPS[1], 0, 0, tiled=True)
 
 
 def width_square(y_gap):
@@ -94,10 +97,10 @@
 
 def split_kernel(v_ref, first_early, last_early, first_late, last_late, first_z, last_z, cells):
     _, nx, nz, _ = v_ref.shape
-    early = first_early.shape[2]
     for k in range(3):
         for j in range(HALO):
             for at, head, tail in ((j, first_early, first_late), (nx - HALO + j, last_early, last_late)):
+                early = head.shape[2]
                 head[k, j] = v_ref[k, at, :early, :]
                 for q in range(tail.shape[2]):
                     row = early + QUAD * q
@@ -228,37 +231,50 @@
     lax.fori_loop(HALO, nx - HALO, result, 0)
 
 
-def outer_kernel(
-    before_early, after_early, before_late, after_late, inv_ref, width_ref,
-    cells_in, filtered_in, smoothed_in, lm_in, mm_in, size_in, totals_in,
-    cells, filtered, smoothed, lm_ref, mm_ref, size_ref, totals, copies,
-    sizes, products,
-):
-    nx, nz, _ = lm_ref.shape
+STATE = 7
+
+
+def outer_pass(layers, inv_ref, width_ref, state, scratch):
+    cells, filtered, smoothed, lm_ref, mm_ref, size_ref, totals = state
+    inverse, width = rows_of(inv_ref), rows_of(width_ref)
+
+    def layer(j, carry):
+        layer_pass(layers[0] + j, inverse, cells, filtered, smoothed, size_ref, *scratch)
+        return carry
+
+    lax.fori_loop(0, HALO, layer, 0, unroll=True)
+
+    def result(j, carry):
+        result_pass(layers[1] + j, inverse, width, filtered, smoothed, lm_ref, mm_ref, totals)
+        return carry
+
+    lax.fori_loop(0, HALO, result, 0, unroll=True)
+
+
+def fill_rim(cells, at, early, late):
+    head, quads = early.shape[2], late.shape[2] - 1
+    end = TOP + head + QUAD * quads
     for j in range(HALO):
-        for at, head, tail in ((j, before_early, before_late), (nx + HALO + j, after_early, after_late)):
-            early, quads = head.shape[2], tail.shape[2] - 1
-            put_layer(cells, at, slice(TOP, TOP + early), lambda k: head[k, j])
-            for q in range(quads):
-                row = TOP + early + QUAD * q
-                put_layer(cells, at, slice(row, row + QUAD), lambda k: tail[k, j, q])
-            put_layer(cells, at, slice(TOP - HALO, TOP), lambda k: tail[k, j, quads, :HALO, :])
-            put_layer(cells, at, slice(TOP + nz, TOP + nz + HALO), lambda k: tail[k, j, quads, HALO:, :])
-    inverse, width = rows_of(inv_ref), rows_of(width_ref)
-
-    def layer(j, carry):
-        i = jnp.where(j < HALO, j, j + nx - HALO)
-        layer_pass(i, inverse, cells, filtered, smoothed, size_ref, sizes, products)
-        return carry
-
-    lax.fori_loop(0, 2 * HALO, layer, 0)
-
-    def result(j, carry):
-        i = jnp.where(j < HALO, j, j + nx - 2 * HALO)
-        result_pass(i, inverse, width, filtered, smoothed, lm_ref, mm_ref, totals)
-        return carry
-
-    lax.fori_loop(0, 2 * HALO, result, 0)
+        put_layer(cells, at + j, slice(TOP, TOP + head), lambda k: early[k, j])
+        for q in range(quads):
+            row = TOP + head + QUAD * q
+            put_layer(cells, at + j, slice(row, row + QUAD), lambda k: late[k, j, q])
+        put_layer(cells, at + j, slice(TOP - HALO, TOP), lambda k: late[k, j, quads, :HALO, :])
+        put_layer(cells, at + j, slice(end, end + HALO), lambda k: late[k, j, quads, HALO:, :])
+
+
+def low_kernel(early, late, inv_ref, width_ref, *refs):
+    state, scratch = refs[STATE : 2 * STATE], refs[2 * STATE :]
+    fill_rim(state[0], 0, early, late)
+    outer_pass((0, 0), inv_ref, width_ref, state, scratch)
+
+
+def high_kernel(early, late, inv_ref, width_ref, *refs):
+    state, copies, scratch = refs[STATE : 2 * STATE], refs[2 * STATE], refs[2 * STATE + 1 :]
+    nx = state[3].shape[0]
+    totals = state[6]
+    fill_rim(state[0], nx + HALO, early, late)
+    outer_pass((nx, nx - HALO), inv_ref, width_ref, state, scratch)
     for n in range(2):
         for c in range(totals.shape[1]):
             line = jnp.sum(totals[n, c], axis=0, keepdims=True)
@@ -315,21 +331,23 @@
 
     cells_shape = (3, nx + 2 * HALO, chunks, rows, LANES)
     field = (nx, nz, ny)
-    quads = (nz - EARLY) // QUAD
+    early = (EARLY_DOWN, EARLY_UP)
     first_early, last_early, first_late, last_late, first_z, last_z, cells = call(
         split_kernel,
-        [(3, HALO, EARLY, ny)] * 2 + [(3, HALO, quads, QUAD, ny)] * 2 + [(3, nx, HALO, ny)] * 2
+        [(3, HALO, e, ny) for e in early] + [(3, HALO, (nz - e) // QUAD, QUAD, ny) for e in early]
+        + [(3, nx, HALO, ny)] * 2
         + [cells_shape],
         [], 0, {}, (velocity,),
     )
-    before_z, after_z = exchange(last_z, first_z, GZ)
-    before_early, after_early = exchange(last_early, first_early, GX)
+    before_z = send(last_z, GZ, 1)
+    after_z = send(first_z, GZ, -1)
+    before_early = send(last_early, GX, 1)
+    after_early = send(first_early, GX, -1)
     near = jnp.concatenate([before_z, after_z], axis=2)[:, :, None]
-    before_late, after_late = exchange(
-        jnp.concatenate([last_late, near[:, nx - HALO :]], axis=2),
-        jnp.concatenate([first_late, near[:, :HALO]], axis=2),
-        GX,
-    )
+    last_late = jnp.concatenate([last_late, near[:, nx - HALO :]], axis=2)
+    first_late = jnp.concatenate([first_late, near[:, :HALO]], axis=2)
+    before_late = send(last_late, GX, 1)
+    after_late = send(first_late, GX, -1)
 
     scratch = [
         pltpu.VMEM((chunks, rows, LANES), jnp.float32),
@@ -346,10 +364,13 @@
         inner_kernel, state_shapes, scratch, 20_000_000, {4: 0},
         (before_z, after_z, *lines, cells),
     )
+    state = call(
+        low_kernel, state_shapes, scratch, 10_000_000,
+        {4 + n: n for n in range(STATE)}, (before_early, before_late, *lines, *state),
+    )
     *state, copies = call(
-        outer_kernel, [*state_shapes, (16, 2, ny)], scratch, 20_000_000,
-        {6 + n: n for n in range(7)},
-        (before_early, after_early, before_late, after_late, *lines, *state),
+        high_kernel, [*state_shapes, (members(GROUPS[0]), 2, ny)], scratch, 10_000_000,
+        {4 + n: n for n in range(STATE)}, (after_early, after_late, *lines, *state),
     )
     lm_field, mm_field, strain_size = state[3:6]
     planes = nx * lax.axis_size(GX) * nz * lax.axis_size(GZ)

time: 57.7 us -> 56.8 us (0.984)
  waiting for transfers between devices: 2.19 us -> 5.93 us
  blocking collectives: 27.2 us -> 24.3 us
  starting transfers between devices: 16.4 us -> 14.8 us
    ppermute x6, waiting for transfers between devices: 2.19 us -> 5.93 us  [send(): lax.ppermute(array, axis, [(i, (i + step) % size) for i in range(size)])]
    all_to_all x2, blocking collectives: 27.2 us -> 24.3 us  [the longest x1 13.3 us: over_axes(): half = jnp.sum(lax.all_to_all(copies, GROUPS[0], 0, 0, tiled=True), axis=0)]
    ppermute x6, starting transfers between devices: 16.4 us -> 14.8 us  [send(): lax.ppermute(array, axis, [(i, (i + step) % size) for i in range(size)])]
    pallas_call x3 -> x4, Pallas kernels: 7.1 us -> 6.89 us  [call(): pl.pallas_call(kernel, out_shape=tuple((pltpu.VMEM(shape, jnp.float32) fo...]
  transfers between devices with their start and end apart: 6 -> 6, of which waited for: 2 -> 2; matrix products, arithmetic and copies ran while one was open for 2% -> 2% of each run, Pallas kernels for 7% -> 9%
where the time goes in v1:
time: 56.8 us; the launch traced here: 56.6 us
  blocking collectives  24.3 us (43%)
  starting transfers between devices  14.8 us (26%)
  Pallas kernels  8.48 us (15%)
  waiting for transfers between devices  5.93 us (10%)
  local copies, waits for them, and re-layouts  1.29 us (2%)
  other arithmetic  1.06 us (2%)
  between operations  0.74 us (1%)
    ppermute x6, starting transfers between devices, send(): lax.ppermute(array, axis, [(i, (i + step) % size) for i in range(size)])  14.8 us
    all_to_all x1, blocking collectives, over_axes(): half = jnp.sum(lax.all_to_all(copies, GROUPS[0], 0, 0, tiled=True), axis=0)  13.3 us
    all_to_all x1, blocking collectives, over_axes(): return lax.all_to_all(copies, GROUPS[1], 0, 0, tiled=True)  11 us
    pallas_call x4, Pallas kernels, call(): pl.pallas_call(kernel, out_shape=tuple((pltpu.VMEM(shape, jnp.float32) fo...  6.89 us
    ppermute x6, waiting for transfers between devices, send(): lax.ppermute(array, axis, [(i, (i + step) % size) for i in range(size)])  5.93 us
    pallas_call x1, Pallas kernels, per_device(): pl.pallas_call(functools.partial(finish_kernel, planes), out_shape=(block...  1.59 us
    unnamed x2, local copies, waits for them, and re-layouts  1.26 us
  transfers between devices with their start and end apart: 6, of which 2 were waited for; matrix products, arithmetic and copies ran while one was open for 2% of the time, Pallas kernels for 9%

profile of v1, /device:TPU:1, one launch (start us, length us, event | category | flops | bytes accessed | tf_op | source)
XLA Modules:
  0.0 56.6 jit_solution(4067881106765088538)
XLA Ops:
  0.6 0.0 copy-start
  0.6 1.3 %copy-done = f32[3,8,32,384]{3,2,1,0:T(8,128)S(1)} copy-done((f32[3,8,32,384]{3,2,1,0:T(8,128)S(1)}, f32[3,8,32,384]{3,2,1,0:T(8,128)}, u32[]{:S(2)}) %copy-start) | copy-done | bytes 1179672
  1.9 0.2 shard_map.57
  2.1 4.2 %collective-permute-start.1 = (f32[3,8,2,384]{3,2,1,0:T(2,128)S(1)}, f32[3,8,2,384]{3,2,1,0:T(2,128)S(1)}, u32[]{:S(2)}, u32[]{:S(2)}) collective-permute-start(f32[3,8,2,384]{3,2,1,0:T(2,128)S(1)} %get-tuple-element.31), channel_id=1, source_target_pairs={{0,1},{1,2},{2,3},{3,4},{4,5},{5,6},{6,7},{7,8},{8,9},{9,10},{10,1... | collective-permute-start | bytes 221192 | tf_op jit(solution)/shard_map/ppermute | solution.py:25
  6.3 0.0 collective-permute-start.2
  6.3 5.6 %collective-permute-start = (f32[3,2,16,384]{3,2,1,0:T(8,128)S(1)}, f32[3,2,16,384]{3,2,1,0:T(8,128)S(1)}, u32[]{:S(2)}, u32[]{:S(2)}) collective-permute-start(f32[3,2,16,384]{3,2,1,0:T(8,128)S(1)} %get-tuple-element.29), channel_id=1, source_target_pairs={{0,240},{16,0},{32,16},{48,32},{64,48},{80,64},{96,80},{112,96},{1... | collective-permute-start | bytes 442376 | tf_op jit(solution)/shard_map/ppermute | solution.py:25
  11.9 0.0 collective-permute-start.4
  11.9 0.0 collective-permute-done.1.before_z
  11.9 2.8 %collective-permute-done.2.after_z = f32[3,8,2,384]{3,2,1,0:T(2,128)S(1)} collective-permute-done((f32[3,8,2,384]{3,2,1,0:T(2,128)S(1)}, f32[3,8,2,384]{3,2,1,0:T(2,128)S(1)}, u32[]{:S(2)}, u32[]{:S(2)}) %collective-permute-start.2) | collective-permute-done | bytes 73760 | tf_op jit(solution)/shard_map/ppermute | solution.py:25
  14.7 0.1 maximum_bitcast_fusion
  14.9 4.9 %collective-permute-start.3 = (f32[3,2,5,4,384]{4,3,2,1,0:T(4,128)S(1)}, f32[3,2,5,4,384]{4,3,2,1,0:T(4,128)S(1)}, u32[]{:S(2)}, u32[]{:S(2)}) collective-permute-start(f32[3,2,5,4,384]{4,3,2,1,0:T(4,128)S(1)} %pad_maximum_fusion), channel_id=1, source_target_pairs={{0,240},{16,0},{32,16},{48,32},{64,48},{80,64},{96,80},{112,96},{1... | collective-permute-start | bytes 552968 | tf_op jit(solution)/shard_map/ppermute | solution.py:25
  19.8 0.1 collective-permute-start.5
  19.9 0.9 %multiply_power_fusion = (f32[384]{0:T(512)S(1)}, f32[384]{0:T(512)S(1)}) fusion(f32[385]{0:T(512)} %param.3), kind=kLoop, calls=%fused_computation.3 | loop fusion | flops 1152 | bytes 6144 | tf_op jit(solution)/shard_map/pow | solution.py:42
  20.8 3.9 %shard_map.58 = (f32[3,12,3,48,128]{4,3,2,1,0:T(8,128)S(1)}, f32[12,10,3,32,128]{4,3,2,1,0:T(8,128)S(1)}, f32[3,10,3,48,128]{4,3,2,1,0:T(8,128)S(1)}, f32[8,32,3...) custom-call(f32[3,8,2,384]{3,2,1,0:T(2,128)S(1)} %collective-permute, ...), custom_call_target="tpu_custom_call", output_to_operand_aliasing={{0}: (4, {})} | custom-call | flops 20000000 | tf_op jit(solution)/shard_map/pallas_call | solution.py:310
  24.7 0.0 collective-permute-done.4.early
  24.7 3.1 %collective-permute-done.5.late = f32[3,2,5,4,384]{4,3,2,1,0:T(4,128)S(1)} collective-permute-done((f32[3,2,5,4,384]{4,3,2,1,0:T(4,128)S(1)}, f32[3,2,5,4,384]{4,3,2,1,0:T(4,128)S(1)}, u32[]{:S(2)}, u32[]{:S(2)}) %collective-permute-start.5) | collective-permute-done | bytes 184352 | tf_op jit(solution)/shard_map/ppermute | solution.py:25
  27.8 1.4 %shard_map.59 = (f32[3,12,3,48,128]{4,3,2,1,0:T(8,128)S(1)}, f32[12,10,3,32,128]{4,3,2,1,0:T(8,128)S(1)}, f32[3,10,3,48,128]{4,3,2,1,0:T(8,128)S(1)}, f32[8,32,3...) custom-call(f32[3,2,16,384]{3,2,1,0:T(8,128)S(1)} %collective-permut, ...), custom_call_target="tpu_custom_call", output_to_operand_aliasing={{0}: (4, {}), {1}: (5, {}), {2}: (6, {}), {3}: (7, {}), {4}... | custom-call | flops 10000000 | tf_op jit(solution)/shard_map/pallas_call | solution.py:310
  29.1 0.0 collective-permute-done.early
  29.2 0.0 collective-permute-done.3.late
  29.2 1.5 %shard_map.60 = (f32[3,12,3,48,128]{4,3,2,1,0:T(8,128)S(1)}, f32[12,10,3,32,128]{4,3,2,1,0:T(8,128)S(1)}, f32[3,10,3,48,128]{4,3,2,1,0:T(8,128)S(1)}, f32[8,32,3...) custom-call(f32[3,2,16,384]{3,2,1,0:T(8,128)S(1)} %collective-permut, ...), custom_call_target="tpu_custom_call", output_to_operand_aliasing={{0}: (4, {}), {1}: (5, {}), {2}: (6, {}), {3}: (7, {}), {4}... | custom-call | flops 10000000 | tf_op jit(solution)/shard_map/pallas_call | solution.py:310
  30.6 13.3 %all_to_all.10 = f32[32,2,384]{2,1,0:T(2,128)S(1)} all-to-all(f32[32,2,384]{2,1,0:T(2,128)S(1)} %get-tuple-element.50), channel_id=1, replica_groups=mesh['gx_0'=8,'gx_1'=2,'gz_0'=4,'gz_1'=2,'gz_2'=2] {'gx_1','gz_0','gz_1'..., dimensions={0} | all-to-all | bytes 196608 | tf_op jit(solution)/shard_map/all_to_all | solution.py:36
  44.0 0.1 reduce_sum.9
  44.0 11.0 %all_to_all.11.parts_ref = f32[8,2,384]{2,1,0:T(2,128)S(1)} all-to-all(f32[8,2,384]{2,1,0:T(2,128)S(1)} %broadcast_in_dim.18), channel_id=1, replica_groups=mesh['gx_0'=8,'gx_1'=2,'gz_0'=4,'gz_1'=2,'gz_2'=2] {'gx_0'}, dimensions={0} | all-to-all | bytes 49152 | tf_op jit(solution)/shard_map/all_to_all | solution.py:38
  55.0 1.6 %finish.1 = (f32[8,32,384]{2,1,0:T(8,128)}, f32[8,32,384]{2,1,0:T(8,128)}, f32[8,32,384]{2,1,0:T(8,128)}, f32[384]{0:T(512)}) custom-call(f32[8,2,384]{2,1,0:T(2,128)S(1)} %all_to_all.11.parts_ref, f32[1,384]{1,0:T(1,128)S(1)} %broadcast_in_dim.17.width_ref, f32[8,32,384]{2,1,0:T(8,128)S(1)} %get-tuple-element.51.lm_ref, ...), custom_call_target="tpu_custom_call" | custom-call | tf_op jit(solution)/shard_map/finish/pallas_call | solution.py:379
  (6 shorter events, 0.1 us)
Async XLA Ops:
  0.6 1.3 %copy-start = (f32[3,8,32,384]{3,2,1,0:T(8,128)S(1)}, f32[3,8,32,384]{3,2,1,0:T(8,128)}, u32[]{:S(2)}) copy-start(f32[3,8,32,384]{3,2,1,0:T(8,128)} %v_ref.1) | copy-start | bytes 3538948
  2.1 9.8 %collective-permute-start.1 = (f32[3,8,2,384]{3,2,1,0:T(2,128)S(1)}, f32[3,8,2,384]{3,2,1,0:T(2,128)S(1)}, u32[]{:S(2)}, u32[]{:S(2)}) collective-permute-start(f32[3,8,2,384]{3,2,1,0:T(2,128)S(1)} %get-tuple-element.31), channel_id=1, source_target_pairs={{0,1},{1,2},{2,3},{3,4},{4,5},{5,6},{6,7},{7,8},{8,9},{9,10},{10,1... | collective-permute-start | bytes 221192 | tf_op jit(solution)/shard_map/ppermute | solution.py:25
  6.3 8.4 %collective-permute-start.2 = (f32[3,8,2,384]{3,2,1,0:T(2,128)S(1)}, f32[3,8,2,384]{3,2,1,0:T(2,128)S(1)}, u32[]{:S(2)}, u32[]{:S(2)}) collective-permute-start(f32[3,8,2,384]{3,2,1,0:T(2,128)S(1)} %get-tuple-element.32), channel_id=1, source_target_pairs={{0,15},{1,0},{2,1},{3,2},{4,3},{5,4},{6,5},{7,6},{8,7},{9,8},{10,9... | collective-permute-start | bytes 221192 | tf_op jit(solution)/shard_map/ppermute | solution.py:25
  6.3 22.9 %collective-permute-start = (f32[3,2,16,384]{3,2,1,0:T(8,128)S(1)}, f32[3,2,16,384]{3,2,1,0:T(8,128)S(1)}, u32[]{:S(2)}, u32[]{:S(2)}) collective-permute-start(f32[3,2,16,384]{3,2,1,0:T(8,128)S(1)} %get-tuple-element.29), channel_id=1, source_target_pairs={{0,240},{16,0},{32,16},{48,32},{64,48},{80,64},{96,80},{112,96},{1... | collective-permute-start | bytes 442376 | tf_op jit(solution)/shard_map/ppermute | solution.py:25
  11.9 12.8 %collective-permute-start.4 = (f32[3,2,16,384]{3,2,1,0:T(8,128)S(1)}, f32[3,2,16,384]{3,2,1,0:T(8,128)S(1)}, u32[]{:S(2)}, u32[]{:S(2)}) collective-permute-start(f32[3,2,16,384]{3,2,1,0:T(8,128)S(1)} %get-tuple-element.33), channel_id=1, source_target_pairs={{0,16},{16,32},{32,48},{48,64},{64,80},{80,96},{96,112},{112,128},... | collective-permute-start | bytes 442376 | tf_op jit(solution)/shard_map/ppermute | solution.py:25
  14.9 14.3 %collective-permute-start.3 = (f32[3,2,5,4,384]{4,3,2,1,0:T(4,128)S(1)}, f32[3,2,5,4,384]{4,3,2,1,0:T(4,128)S(1)}, u32[]{:S(2)}, u32[]{:S(2)}) collective-permute-start(f32[3,2,5,4,384]{4,3,2,1,0:T(4,128)S(1)} %pad_maximum_fusion), channel_id=1, source_target_pairs={{0,240},{16,0},{32,16},{48,32},{64,48},{80,64},{96,80},{112,96},{1... | collective-permute-start | bytes 552968 | tf_op jit(solution)/shard_map/ppermute | solution.py:25
  19.8 8.0 %collective-permute-start.5 = (f32[3,2,5,4,384]{4,3,2,1,0:T(4,128)S(1)}, f32[3,2,5,4,384]{4,3,2,1,0:T(4,128)S(1)}, u32[]{:S(2)}, u32[]{:S(2)}) collective-permute-start(f32[3,2,5,4,384]{4,3,2,1,0:T(4,128)S(1)} %pad_maximum_fusion.1), channel_id=1, source_target_pairs={{0,16},{16,32},{32,48},{48,64},{64,80},{80,96},{96,112},{112,128},... | collective-permute-start | bytes 552968 | tf_op jit(solution)/shard_map/ppermute | solution.py:25

commit v2 on v1

--- a/solution.py
+++ b/solution.py
@@ -16,13 +16,21 @@
 SUB = 8
 TOP = 8
 HALO = 2
-EARLY_UP, EARLY_DOWN = 16, 16
+EARLY_UP, EARLY_DOWN = 24, 24
 QUAD = 2 * HALO
 
 
-def send(array, axis, step):
+def send(array, axis, target):
     size = lax.axis_size(axis)
-    return lax.ppermute(array, axis, [(i, (i + step) % size) for i in range(size)])
+    return lax.ppermute(array, axis, [(i, target(i) % size) for i in range(size)])
+
+
+def is_odd():
+    return lax.axis_index("gz_2") == 1
+
+
+def pick(odd, if_odd, if_even):
+    return jnp.where(odd, if_odd, if_even)
 
 
 GROUPS = (("gx_1", "gz_0", "gz_1", "gz_2"), ("gx_0",))
@@ -95,8 +103,9 @@
             cells[k, at, c, rows, :] = value(k)[:, column(c)]
 
 
-def split_kernel(v_ref, first_early, last_early, first_late, last_late, first_z, last_z, cells):
+def split_kernel(v_ref, first_early, last_early, first_late, last_late, across, within, cells):
     _, nx, nz, _ = v_ref.shape
+    odd = is_odd()
     for k in range(3):
         for j in range(HALO):
             for at, head, tail in ((j, first_early, first_late), (nx - HALO + j, last_early, last_late)):
@@ -106,14 +115,29 @@
                     row = early + QUAD * q
                     tail[k, j, q] = v_ref[k, at, row : row + QUAD, :]
         for i in range(nx):
-            first_z[k, i] = v_ref[k, i, :HALO, :]
-            last_z[k, i] = v_ref[k, i, nz - HALO :, :]
+            first, last = v_ref[k, i, :HALO, :], v_ref[k, i, nz - HALO :, :]
+            across[k, i] = pick(odd, last, first)
+            within[k, i] = pick(odd, first, last)
 
     def own(i, carry):
         put_layer(cells, i + HALO, slice(TOP, TOP + nz), lambda k: v_ref[k, i])
         return carry
 
     lax.fori_loop(0, nx, own, 0)
+
+
+def join_kernel(across, within, first_late, last_late, first_out, last_out):
+    nx = across.shape[1]
+    odd = is_odd()
+    for k in range(3):
+        for j in range(HALO):
+            for at, late, out in ((j, first_late, first_out), (nx - HALO + j, last_late, last_out)):
+                quads = late.shape[2]
+                for q in range(quads):
+                    out[k, j, q] = late[k, j, q]
+                there, here = across[k, at], within[k, at]
+                out[k, j, quads, :HALO, :] = pick(odd, here, there)
+                out[k, j, quads, HALO:, :] = pick(odd, there, here)
 
 
 def layer_pass(i, inverse, cells, filtered, smoothed, size_ref, sizes, products):
@@ -203,15 +227,18 @@
 
 
 def inner_kernel(
-    before_z, after_z, inv_ref, width_ref, cells_in,
+    across, within, inv_ref, width_ref, cells_in,
     cells, filtered, smoothed, lm_ref, mm_ref, size_ref, totals,
     sizes, products,
 ):
     nx, nz, _ = lm_ref.shape
 
+    odd = is_odd()
+
     def sides(i, carry):
-        put_layer(cells, i + HALO, slice(TOP - HALO, TOP), lambda k: before_z[k, i])
-        put_layer(cells, i + HALO, slice(TOP + nz, TOP + nz + HALO), lambda k: after_z[k, i])
+        for rows, flip in ((slice(TOP - HALO, TOP), False), (slice(TOP + nz, TOP + nz + HALO), True)):
+            there, here = (across, within) if flip else (within, across)
+            put_layer(cells, i + HALO, rows, lambda k: pick(odd, there[k, i], here[k, i]))
         return carry
 
     lax.fori_loop(0, nx, sides, 0)
@@ -270,9 +297,16 @@
 
 
 def high_kernel(early, late, inv_ref, width_ref, *refs):
-    state, copies, scratch = refs[STATE : 2 * STATE], refs[2 * STATE], refs[2 * STATE + 1 :]
+    state, (copies, lm_out, mm_out, *scratch, sems) = refs[STATE : 2 * STATE], refs[2 * STATE :]
     nx = state[3].shape[0]
     totals = state[6]
+    ready = pl.ds(0, nx - HALO)
+    stores = [
+        pltpu.make_async_copy(state[3 + n].at[ready], out.at[ready], sems.at[n])
+        for n, out in enumerate((lm_out, mm_out))
+    ]
+    for store in stores:
+        store.start()
     fill_rim(state[0], nx + HALO, early, late)
     outer_pass((nx, nx - HALO), inv_ref, width_ref, state, scratch)
     for n in range(2):
@@ -280,38 +314,51 @@
             line = jnp.sum(totals[n, c], axis=0, keepdims=True)
             for member in range(copies.shape[0]):
                 copies[member, n : n + 1, column(c)] = line
+    for store in stores:
+        store.wait()
 
 
 def finish_kernel(
-    planes, parts_ref, width_ref, lm_ref, mm_ref, size_ref,
+    planes, parts_ref, width_ref, lm_ref, mm_ref, size_ref, lm_in, mm_in,
     eddy_out, lm_out, mm_out, coefficient_ref,
     eddy_ref, sems,
 ):
+    nx = lm_ref.shape[0]
+    last = pl.ds(nx - HALO, HALO)
     stores = [
-        pltpu.make_async_copy(lm_ref, lm_out, sems.at[0]),
-        pltpu.make_async_copy(mm_ref, mm_out, sems.at[1]),
-        pltpu.make_async_copy(eddy_ref, eddy_out, sems.at[2]),
-    ]
-    stores[0].start()
-    stores[1].start()
+        pltpu.make_async_copy(ref.at[last], out.at[last], sems.at[n])
+        for n, (ref, out) in enumerate(((lm_ref, lm_out), (mm_ref, mm_out)))
+    ]
+    for store in stores:
+        store.start()
     total = parts_ref[0]
     for member in range(1, parts_ref.shape[0]):
         total = total + parts_ref[member]
     coefficient = total[0:1] / planes / (total[1:2] / planes + 1e-06)
     coefficient_ref[...] = coefficient[0]
-    eddy_ref[...] = (coefficient * width_ref[...])[None] * size_ref[...]
-    stores[2].start()
+    scale = (coefficient * width_ref[...])[None]
+    for n in range(nx // HALO):
+        part = pl.ds(HALO * n, HALO)
+        eddy_ref[part] = scale * size_ref[part]
+        stores.append(pltpu.make_async_copy(eddy_ref.at[part], eddy_out.at[part], sems.at[2 + n]))
+        stores[-1].start()
     for store in stores:
         store.wait()
 
 
-def call(kernel, outs, scratch, flops, aliases, args):
-    whole = pl.BlockSpec(memory_space=pltpu.VMEM)
+WHOLE = pl.BlockSpec(memory_space=pltpu.VMEM)
+THERE = pl.BlockSpec(memory_space=pl.ANY)
+
+
+def call(kernel, outs, scratch, flops, aliases, args, stored=()):
     return pl.pallas_call(
         kernel,
-        out_shape=tuple(pltpu.VMEM(shape, jnp.float32) for shape in outs),
-        in_specs=[whole] * len(args),
-        out_specs=tuple([whole] * len(outs)),
+        out_shape=(
+            *[pltpu.VMEM(shape, jnp.float32) for shape in outs],
+            *[jax.ShapeDtypeStruct(shape, jnp.float32) for shape in stored],
+        ),
+        in_specs=[WHOLE] * len(args),
+        out_specs=(*[WHOLE] * len(outs), *[THERE] * len(stored)),
         scratch_shapes=scratch,
         input_output_aliases=aliases,
         cost_estimate=pl.CostEstimate(flops=flops, bytes_accessed=0, transcendentals=0),
@@ -332,22 +379,23 @@
     cells_shape = (3, nx + 2 * HALO, chunks, rows, LANES)
     field = (nx, nz, ny)
     early = (EARLY_DOWN, EARLY_UP)
-    first_early, last_early, first_late, last_late, first_z, last_z, cells = call(
+    first_early, last_early, first_late, last_late, across, within, cells = call(
         split_kernel,
         [(3, HALO, e, ny) for e in early] + [(3, HALO, (nz - e) // QUAD, QUAD, ny) for e in early]
         + [(3, nx, HALO, ny)] * 2
         + [cells_shape],
         [], 0, {}, (velocity,),
     )
-    before_z = send(last_z, GZ, 1)
-    after_z = send(first_z, GZ, -1)
-    before_early = send(last_early, GX, 1)
-    after_early = send(first_early, GX, -1)
-    near = jnp.concatenate([before_z, after_z], axis=2)[:, :, None]
-    last_late = jnp.concatenate([last_late, near[:, nx - HALO :]], axis=2)
-    first_late = jnp.concatenate([first_late, near[:, :HALO]], axis=2)
-    before_late = send(last_late, GX, 1)
-    after_late = send(first_late, GX, -1)
+    across = send(across, GZ, lambda i: i + 1 if i % 2 else i - 1)
+    within = send(within, GZ, lambda i: i - 1 if i % 2 else i + 1)
+    before_early = send(last_early, GX, lambda i: i + 1)
+    after_early = send(first_early, GX, lambda i: i - 1)
+    first_late, last_late = call(
+        join_kernel, [(3, HALO, nz // QUAD - e // QUAD + 1, QUAD, ny) for e in early],
+        [], 0, {}, (across, within, first_late, last_late),
+    )
+    before_late = send(last_late, GX, lambda i: i + 1)
+    after_late = send(first_late, GX, lambda i: i - 1)
 
     scratch = [
         pltpu.VMEM((chunks, rows, LANES), jnp.float32),
@@ -362,29 +410,30 @@
     ]
     state = call(
         inner_kernel, state_shapes, scratch, 20_000_000, {4: 0},
-        (before_z, after_z, *lines, cells),
+        (across, within, *lines, cells),
     )
     state = call(
         low_kernel, state_shapes, scratch, 10_000_000,
         {4 + n: n for n in range(STATE)}, (before_early, before_late, *lines, *state),
     )
-    *state, copies = call(
-        high_kernel, [*state_shapes, (members(GROUPS[0]), 2, ny)], scratch, 10_000_000,
-        {4 + n: n for n in range(STATE)}, (after_early, after_late, *lines, *state),
+    *state, copies, lm_out, mm_out = call(
+        high_kernel, [*state_shapes, (members(GROUPS[0]), 2, ny)],
+        [*scratch, pltpu.SemaphoreType.DMA((2,))], 10_000_000,
+        {4 + n: n for n in range(STATE)}, (after_early, after_late, *lines, *state), [field] * 2,
     )
     lm_field, mm_field, strain_size = state[3:6]
     planes = nx * lax.axis_size(GX) * nz * lax.axis_size(GZ)
-    whole, there = pl.BlockSpec(memory_space=pltpu.VMEM), pl.BlockSpec(memory_space=pl.ANY)
     block = jax.ShapeDtypeStruct(field, jnp.float32)
     eddy_visc, lm_field, mm_field, coefficient = pl.pallas_call(
         functools.partial(finish_kernel, planes),
         out_shape=(block, block, block, jax.ShapeDtypeStruct((ny,), jnp.float32)),
-        in_specs=[whole] * 5,
-        out_specs=(there, there, there, whole),
-        scratch_shapes=[pltpu.VMEM(field, jnp.float32), pltpu.SemaphoreType.DMA((3,))],
+        in_specs=[WHOLE] * 5 + [THERE] * 2,
+        out_specs=(THERE, THERE, THERE, WHOLE),
+        scratch_shapes=[pltpu.VMEM(field, jnp.float32), pltpu.SemaphoreType.DMA((2 + nx // HALO,))],
+        input_output_aliases={5: 1, 6: 2},
         name="finish",
         compiler_params=pltpu.CompilerParams(vmem_limit_bytes=VMEM_LIMIT),
-    )(over_axes(copies), lines[1], lm_field, mm_field, strain_size)
+    )(over_axes(copies), lines[1], lm_field, mm_field, strain_size, lm_out, mm_out)
     return (eddy_visc, lm_field, mm_field, coefficient)
 
 

time: 56.8 us -> 57.3 us (level)
  waiting for transfers between devices: 5.93 us -> 2.75 us
  blocking collectives: 24.3 us -> 27.3 us
  starting transfers between devices: 14.8 us -> 15.7 us
    ppermute x6, waiting for transfers between devices: 5.93 us -> 2.75 us  [send(): lax.ppermute(array, axis, [(i, target(i) % size) for i in range(size)])]
    all_to_all x1, blocking collectives: 11 us -> 13.5 us  [over_axes(): return lax.all_to_all(copies, GROUPS[1], 0, 0, tiled=True)]
    ppermute x6, starting transfers between devices: 14.8 us -> 15.7 us  [send(): lax.ppermute(array, axis, [(i, target(i) % size) for i in range(size)])]
    pallas_call x4 -> x5, Pallas kernels: 6.89 us -> 6.98 us  [call(): pl.pallas_call(kernel, out_shape=(*[pltpu.VMEM(shape, jnp.float32) for sh...]
  transfers between devices with their start and end apart: 6 -> 6, of which waited for: 2 -> 1; matrix products, arithmetic and copies ran while one was open for 2% -> 1% of each run, Pallas kernels for 9% -> 9%
where the time goes in v2:
time: 57.3 us; the launch traced here: 57.1 us
  blocking collectives  27.3 us (48%)
  starting transfers between devices  15.7 us (27%)
  Pallas kernels  8.4 us (15%)
  waiting for transfers between devices  2.75 us (5%)
  local copies, waits for them, and re-layouts  1.28 us (2%)
  other arithmetic  0.9 us (2%)
  between operations  0.71 us (1%)
    ppermute x6, starting transfers between devices, send(): lax.ppermute(array, axis, [(i, target(i) % size) for i in range(size)])  15.7 us
    all_to_all x1, blocking collectives, over_axes(): half = jnp.sum(lax.all_to_all(copies, GROUPS[0], 0, 0, tiled=True), axis=0)  13.8 us
    all_to_all x1, blocking collectives, over_axes(): return lax.all_to_all(copies, GROUPS[1], 0, 0, tiled=True)  13.5 us
    pallas_call x5, Pallas kernels, call(): pl.pallas_call(kernel, out_shape=(*[pltpu.VMEM(shape, jnp.float32) for sh...  6.98 us
    ppermute x6, waiting for transfers between devices, send(): lax.ppermute(array, axis, [(i, target(i) % size) for i in range(size)])  2.75 us
    pallas_call x1, Pallas kernels, per_device(): pl.pallas_call(functools.partial(finish_kernel, planes), out_shape=(block...  1.42 us
    unnamed x2, local copies, waits for them, and re-layouts  1.26 us
  transfers between devices with their start and end apart: 6, of which 1 were waited for; matrix products, arithmetic and copies ran while one was open for 1% of the time, Pallas kernels for 9%

profile of v2, /device:TPU:1, one launch (start us, length us, event | category | flops | bytes accessed | tf_op | source)
XLA Modules:
  0.0 57.1 jit_solution(7169729814839447762)
XLA Ops:
  0.6 0.0 copy-start
  0.6 1.3 %copy-done = f32[3,8,32,384]{3,2,1,0:T(8,128)S(1)} copy-done((f32[3,8,32,384]{3,2,1,0:T(8,128)S(1)}, f32[3,8,32,384]{3,2,1,0:T(8,128)}, u32[]{:S(2)}) %copy-start) | copy-done | bytes 1179672
  1.9 0.2 shard_map.57
  2.1 4.2 %collective-permute-start.1 = (f32[3,8,2,384]{3,2,1,0:T(2,128)S(1)}, f32[3,8,2,384]{3,2,1,0:T(2,128)S(1)}, u32[]{:S(2)}, u32[]{:S(2)}) collective-permute-start(f32[3,8,2,384]{3,2,1,0:T(2,128)S(1)} %get-tuple-element.34), channel_id=1, source_target_pairs={{0,15},{1,2},{2,1},{3,4},{4,3},{5,6},{6,5},{7,8},{8,7},{9,10},{10,... | collective-permute-start | bytes 221192 | tf_op jit(solution)/shard_map/ppermute | solution.py:25
  6.3 2.3 %collective-permute-start.2 = (f32[3,8,2,384]{3,2,1,0:T(2,128)S(1)}, f32[3,8,2,384]{3,2,1,0:T(2,128)S(1)}, u32[]{:S(2)}, u32[]{:S(2)}) collective-permute-start(f32[3,8,2,384]{3,2,1,0:T(2,128)S(1)} %get-tuple-element.35), channel_id=1, source_target_pairs={{0,1},{1,0},{2,3},{3,2},{4,5},{5,4},{6,7},{7,6},{8,9},{9,8},{10,11... | collective-permute-start | bytes 221192 | tf_op jit(solution)/shard_map/ppermute | solution.py:25
  8.6 5.6 %collective-permute-start = (f32[3,2,24,384]{3,2,1,0:T(8,128)S(1)}, f32[3,2,24,384]{3,2,1,0:T(8,128)S(1)}, u32[]{:S(2)}, u32[]{:S(2)}) collective-permute-start(f32[3,2,24,384]{3,2,1,0:T(8,128)S(1)} %get-tuple-element.33), channel_id=1, source_target_pairs={{0,240},{16,0},{32,16},{48,32},{64,48},{80,64},{96,80},{112,96},{1... | collective-permute-start | bytes 663560 | tf_op jit(solution)/shard_map/ppermute | solution.py:25
  14.2 0.0 collective-permute-start.4
  14.2 0.0 collective-permute-done.1.across
  14.2 0.0 collective-permute-done.2.within
  14.3 3.6 %collective-permute-start.3 = (f32[3,2,3,4,384]{4,3,2,1,0:T(4,128)S(1)}, f32[3,2,3,4,384]{4,3,2,1,0:T(4,128)S(1)}, u32[]{:S(2)}, u32[]{:S(2)}) collective-permute-start(f32[3,2,3,4,384]{4,3,2,1,0:T(4,128)S(1)} %get-tuple-element.38), channel_id=1, source_target_pairs={{0,240},{16,0},{32,16},{48,32},{64,48},{80,64},{96,80},{112,96},{1... | collective-permute-start | bytes 331784 | tf_op jit(solution)/shard_map/ppermute | solution.py:25
  17.9 0.0 collective-permute-start.5
  17.9 0.8 %multiply_power_fusion = (f32[384]{0:T(512)S(1)}, f32[384]{0:T(512)S(1)}) fusion(f32[385]{0:T(512)} %param.3), kind=kLoop, calls=%fused_computation | loop fusion | flops 1152 | bytes 6144 | tf_op jit(solution)/shard_map/pow | solution.py:50
  18.8 3.9 %shard_map.59 = (f32[3,12,3,48,128]{4,3,2,1,0:T(8,128)S(1)}, f32[12,10,3,32,128]{4,3,2,1,0:T(8,128)S(1)}, f32[3,10,3,48,128]{4,3,2,1,0:T(8,128)S(1)}, f32[8,32,3...) custom-call(f32[3,8,2,384]{3,2,1,0:T(2,128)S(1)} %collective-permute, ...), custom_call_target="tpu_custom_call", output_to_operand_aliasing={{0}: (4, {})} | custom-call | flops 20000000 | tf_op jit(solution)/shard_map/pallas_call | solution.py:354
  22.7 2.7 %collective-permute-done.5.late = f32[3,2,3,4,384]{4,3,2,1,0:T(4,128)S(1)} collective-permute-done((f32[3,2,3,4,384]{4,3,2,1,0:T(4,128)S(1)}, f32[3,2,3,4,384]{4,3,2,1,0:T(4,128)S(1)}, u32[]{:S(2)}, u32[]{:S(2)}) %collective-permute-start.5) | collective-permute-done | bytes 110624 | tf_op jit(solution)/shard_map/ppermute | solution.py:25
  25.4 0.0 collective-permute-done.4.early
  25.4 1.4 %shard_map.60 = (f32[3,12,3,48,128]{4,3,2,1,0:T(8,128)S(1)}, f32[12,10,3,32,128]{4,3,2,1,0:T(8,128)S(1)}, f32[3,10,3,48,128]{4,3,2,1,0:T(8,128)S(1)}, f32[8,32,3...) custom-call(f32[3,2,24,384]{3,2,1,0:T(8,128)S(1)} %collective-permut, ...), custom_call_target="tpu_custom_call", output_to_operand_aliasing={{0}: (4, {}), {1}: (5, {}), {2}: (6, {}), {3}: (7, {}), {4}... | custom-call | flops 10000000 | tf_op jit(solution)/shard_map/pallas_call | solution.py:354
  26.8 0.0 collective-permute-done.3.late
  26.8 0.0 collective-permute-done.early
  26.8 1.5 %shard_map.61 = (f32[3,12,3,48,128]{4,3,2,1,0:T(8,128)S(1)}, f32[12,10,3,32,128]{4,3,2,1,0:T(8,128)S(1)}, f32[3,10,3,48,128]{4,3,2,1,0:T(8,128)S(1)}, f32[8,32,3...) custom-call(f32[3,2,24,384]{3,2,1,0:T(8,128)S(1)} %collective-permut, ...), custom_call_target="tpu_custom_call", output_to_operand_aliasing={{0}: (4, {}), {1}: (5, {}), {2}: (6, {}), {3}: (7, {}), {4}... | custom-call | flops 10000000 | tf_op jit(solution)/shard_map/pallas_call | solution.py:354
  28.3 13.8 %all_to_all.10 = f32[32,2,384]{2,1,0:T(2,128)S(1)} all-to-all(f32[32,2,384]{2,1,0:T(2,128)S(1)} %get-tuple-element.56), channel_id=1, replica_groups=mesh['gx_0'=8,'gx_1'=2,'gz_0'=4,'gz_1'=2,'gz_2'=2] {'gx_1','gz_0','gz_1'..., dimensions={0} | all-to-all | bytes 196608 | tf_op jit(solution)/shard_map/all_to_all | solution.py:44
  42.2 0.1 reduce_sum.9
  42.2 13.5 %all_to_all.11.parts_ref = f32[8,2,384]{2,1,0:T(2,128)S(1)} all-to-all(f32[8,2,384]{2,1,0:T(2,128)S(1)} %broadcast_in_dim.14), channel_id=1, replica_groups=mesh['gx_0'=8,'gx_1'=2,'gz_0'=4,'gz_1'=2,'gz_2'=2] {'gx_0'}, dimensions={0} | all-to-all | bytes 49152 | tf_op jit(solution)/shard_map/all_to_all | solution.py:46
  55.7 1.4 %finish.1 = (f32[8,32,384]{2,1,0:T(8,128)}, f32[8,32,384]{2,1,0:T(8,128)}, f32[8,32,384]{2,1,0:T(8,128)}, f32[384]{0:T(512)}) custom-call(f32[8,2,384]{2,1,0:T(2,128)S(1)} %all_to_all.11.parts_ref, f32[1,384]{1,0:T(1,128)S(1)} %broadcast_in_dim.13.width_ref, ...), custom_call_target="tpu_custom_call", output_to_operand_aliasing={{1}: (5, {}), {2}: (6, {})} | custom-call | tf_op jit(solution)/shard_map/finish/pallas_call | solution.py:427
  (4 shorter events, 0.1 us)
Async XLA Ops:
  0.6 1.3 %copy-start = (f32[3,8,32,384]{3,2,1,0:T(8,128)S(1)}, f32[3,8,32,384]{3,2,1,0:T(8,128)}, u32[]{:S(2)}) copy-start(f32[3,8,32,384]{3,2,1,0:T(8,128)} %v_ref.1) | copy-start | bytes 3538948
  2.1 12.1 %collective-permute-start.1 = (f32[3,8,2,384]{3,2,1,0:T(2,128)S(1)}, f32[3,8,2,384]{3,2,1,0:T(2,128)S(1)}, u32[]{:S(2)}, u32[]{:S(2)}) collective-permute-start(f32[3,8,2,384]{3,2,1,0:T(2,128)S(1)} %get-tuple-element.34), channel_id=1, source_target_pairs={{0,15},{1,2},{2,1},{3,4},{4,3},{5,6},{6,5},{7,8},{8,7},{9,10},{10,... | collective-permute-start | bytes 221192 | tf_op jit(solution)/shard_map/ppermute | solution.py:25
  6.3 7.9 %collective-permute-start.2 = (f32[3,8,2,384]{3,2,1,0:T(2,128)S(1)}, f32[3,8,2,384]{3,2,1,0:T(2,128)S(1)}, u32[]{:S(2)}, u32[]{:S(2)}) collective-permute-start(f32[3,8,2,384]{3,2,1,0:T(2,128)S(1)} %get-tuple-element.35), channel_id=1, source_target_pairs={{0,1},{1,0},{2,3},{3,2},{4,5},{5,4},{6,7},{7,6},{8,9},{9,8},{10,11... | collective-permute-start | bytes 221192 | tf_op jit(solution)/shard_map/ppermute | solution.py:25
  8.6 18.2 %collective-permute-start = (f32[3,2,24,384]{3,2,1,0:T(8,128)S(1)}, f32[3,2,24,384]{3,2,1,0:T(8,128)S(1)}, u32[]{:S(2)}, u32[]{:S(2)}) collective-permute-start(f32[3,2,24,384]{3,2,1,0:T(8,128)S(1)} %get-tuple-element.33), channel_id=1, source_target_pairs={{0,240},{16,0},{32,16},{48,32},{64,48},{80,64},{96,80},{112,96},{1... | collective-permute-start | bytes 663560 | tf_op jit(solution)/shard_map/ppermute | solution.py:25
  14.2 11.2 %collective-permute-start.4 = (f32[3,2,24,384]{3,2,1,0:T(8,128)S(1)}, f32[3,2,24,384]{3,2,1,0:T(8,128)S(1)}, u32[]{:S(2)}, u32[]{:S(2)}) collective-permute-start(f32[3,2,24,384]{3,2,1,0:T(8,128)S(1)} %get-tuple-element.39), channel_id=1, source_target_pairs={{0,16},{16,32},{32,48},{48,64},{64,80},{80,96},{96,112},{112,128},... | collective-permute-start | bytes 663560 | tf_op jit(solution)/shard_map/ppermute | solution.py:25
  14.3 12.5 %collective-permute-start.3 = (f32[3,2,3,4,384]{4,3,2,1,0:T(4,128)S(1)}, f32[3,2,3,4,384]{4,3,2,1,0:T(4,128)S(1)}, u32[]{:S(2)}, u32[]{:S(2)}) collective-permute-start(f32[3,2,3,4,384]{4,3,2,1,0:T(4,128)S(1)} %get-tuple-element.38), channel_id=1, source_target_pairs={{0,240},{16,0},{32,16},{48,32},{64,48},{80,64},{96,80},{112,96},{1... | collective-permute-start | bytes 331784 | tf_op jit(solution)/shard_map/ppermute | solution.py:25
  17.9 7.5 %collective-permute-start.5 = (f32[3,2,3,4,384]{4,3,2,1,0:T(4,128)S(1)}, f32[3,2,3,4,384]{4,3,2,1,0:T(4,128)S(1)}, u32[]{:S(2)}, u32[]{:S(2)}) collective-permute-start(f32[3,2,3,4,384]{4,3,2,1,0:T(4,128)S(1)} %get-tuple-element.40), channel_id=1, source_target_pairs={{0,16},{16,32},{32,48},{48,64},{64,80},{80,96},{96,112},{112,128},... | collective-permute-start | bytes 331784 | tf_op jit(solution)/shard_map/ppermute | solution.py:25

commit v3 on v2

--- a/solution.py
+++ b/solution.py
@@ -103,7 +103,7 @@
             cells[k, at, c, rows, :] = value(k)[:, column(c)]
 
 
-def split_kernel(v_ref, first_early, last_early, first_late, last_late, across, within, cells):
+def split_kernel(v_ref, first_early, last_early, first_late, last_late, across, within):
     _, nx, nz, _ = v_ref.shape
     odd = is_odd()
     for k in range(3):
@@ -118,12 +118,6 @@
             first, last = v_ref[k, i, :HALO, :], v_ref[k, i, nz - HALO :, :]
             across[k, i] = pick(odd, last, first)
             within[k, i] = pick(odd, first, last)
-
-    def own(i, carry):
-        put_layer(cells, i + HALO, slice(TOP, TOP + nz), lambda k: v_ref[k, i])
-        return carry
-
-    lax.fori_loop(0, nx, own, 0)
 
 
 def join_kernel(across, within, first_late, last_late, first_out, last_out):
@@ -227,7 +221,7 @@
 
 
 def inner_kernel(
-    across, within, inv_ref, width_ref, cells_in,
+    across, within, inv_ref, width_ref, v_ref,
     cells, filtered, smoothed, lm_ref, mm_ref, size_ref, totals,
     sizes, products,
 ):
@@ -236,6 +230,7 @@
     odd = is_odd()
 
     def sides(i, carry):
+        put_layer(cells, i + HALO, slice(TOP, TOP + nz), lambda k: v_ref[k, i])
         for rows, flip in ((slice(TOP - HALO, TOP), False), (slice(TOP + nz, TOP + nz + HALO), True)):
             there, here = (across, within) if flip else (within, across)
             put_layer(cells, i + HALO, rows, lambda k: pick(odd, there[k, i], here[k, i]))
@@ -379,11 +374,10 @@
     cells_shape = (3, nx + 2 * HALO, chunks, rows, LANES)
     field = (nx, nz, ny)
     early = (EARLY_DOWN, EARLY_UP)
-    first_early, last_early, first_late, last_late, across, within, cells = call(
+    first_early, last_early, first_late, last_late, across, within = call(
         split_kernel,
         [(3, HALO, e, ny) for e in early] + [(3, HALO, (nz - e) // QUAD, QUAD, ny) for e in early]
-        + [(3, nx, HALO, ny)] * 2
-        + [cells_shape],
+        + [(3, nx, HALO, ny)] * 2,
         [], 0, {}, (velocity,),
     )
     across = send(across, GZ, lambda i: i + 1 if i % 2 else i - 1)
@@ -409,8 +403,8 @@
         (2, chunks, SUB, LANES),
     ]
     state = call(
-        inner_kernel, state_shapes, scratch, 20_000_000, {4: 0},
-        (across, within, *lines, cells),
+        inner_kernel, state_shapes, scratch, 20_000_000, {},
+        (across, within, *lines, velocity),
     )
     state = call(
         low_kernel, state_shapes, scratch, 10_000_000,

time: 57.3 us -> 58.4 us (1.019)
  local copies, waits for them, and re-layouts: 1.28 us -> 2.55 us
  waiting for transfers between devices: 2.75 us -> 1.51 us
  blocking collectives: 27.3 us -> 28.4 us
    unnamed x2 -> x4, local copies, waits for them, and re-layouts: 1.26 us -> 2.53 us
    ppermute x6, waiting for transfers between devices: 2.75 us -> 1.51 us  [send(): lax.ppermute(array, axis, [(i, target(i) % size) for i in range(size)])]
    all_to_all x1, blocking collectives: 13.5 us -> 14.6 us  [over_axes(): return lax.all_to_all(copies, GROUPS[1], 0, 0, tiled=True)]
where the time goes in v3:
time: 58.4 us; the launch traced here: 58.2 us
  blocking collectives  28.4 us (49%)
  starting transfers between devices  15.7 us (27%)
  Pallas kernels  8.3 us (14%)
  local copies, waits for them, and re-layouts  2.55 us (4%)
  waiting for transfers between devices  1.51 us (3%)
  other arithmetic  0.9 us (2%)
  between operations  0.72 us (1%)
    ppermute x6, starting transfers between devices, send(): lax.ppermute(array, axis, [(i, target(i) % size) for i in range(size)])  15.7 us
    all_to_all x1, blocking collectives, over_axes(): return lax.all_to_all(copies, GROUPS[1], 0, 0, tiled=True)  14.6 us
    all_to_all x1, blocking collectives, over_axes(): half = jnp.sum(lax.all_to_all(copies, GROUPS[0], 0, 0, tiled=True), axis=0)  13.8 us
    pallas_call x5, Pallas kernels, call(): pl.pallas_call(kernel, out_shape=(*[pltpu.VMEM(shape, jnp.float32) for sh...  6.88 us
    unnamed x4, local copies, waits for them, and re-layouts  2.53 us
    ppermute x6, waiting for transfers between devices, send(): lax.ppermute(array, axis, [(i, target(i) % size) for i in range(size)])  1.51 us
    pallas_call x1, Pallas kernels, per_device(): pl.pallas_call(functools.partial(finish_kernel, planes), out_shape=(block...  1.42 us
  transfers between devices with their start and end apart: 6, of which 1 were waited for; matrix products, arithmetic and copies ran while one was open for 1% of the time, Pallas kernels for 9%

profile of v3, /device:TPU:1, one launch (start us, length us, event | category | flops | bytes accessed | tf_op | source)
XLA Modules:
  0.0 58.2 jit_solution(5622896032973225039)
XLA Ops:
  0.6 0.0 copy-start
  0.6 1.3 %copy-done = f32[3,8,32,384]{3,2,1,0:T(8,128)S(1)} copy-done((f32[3,8,32,384]{3,2,1,0:T(8,128)S(1)}, f32[3,8,32,384]{3,2,1,0:T(8,128)}, u32[]{:S(2)}) %copy-start) | copy-done | bytes 1179672
  1.9 0.1 shard_map.57
  2.0 4.2 %collective-permute-start.1 = (f32[3,8,2,384]{3,2,1,0:T(2,128)S(1)}, f32[3,8,2,384]{3,2,1,0:T(2,128)S(1)}, u32[]{:S(2)}, u32[]{:S(2)}) collective-permute-start(f32[3,8,2,384]{3,2,1,0:T(2,128)S(1)} %get-tuple-element.33), channel_id=1, source_target_pairs={{0,15},{1,2},{2,1},{3,4},{4,3},{5,6},{6,5},{7,8},{8,7},{9,10},{10,... | collective-permute-start | bytes 221192 | tf_op jit(solution)/shard_map/ppermute | solution.py:25
  6.2 2.3 %collective-permute-start.2 = (f32[3,8,2,384]{3,2,1,0:T(2,128)S(1)}, f32[3,8,2,384]{3,2,1,0:T(2,128)S(1)}, u32[]{:S(2)}, u32[]{:S(2)}) collective-permute-start(f32[3,8,2,384]{3,2,1,0:T(2,128)S(1)} %get-tuple-element.34), channel_id=1, source_target_pairs={{0,1},{1,0},{2,3},{3,2},{4,5},{5,4},{6,7},{7,6},{8,9},{9,8},{10,11... | collective-permute-start | bytes 221192 | tf_op jit(solution)/shard_map/ppermute | solution.py:25
  8.5 5.6 %collective-permute-start = (f32[3,2,24,384]{3,2,1,0:T(8,128)S(1)}, f32[3,2,24,384]{3,2,1,0:T(8,128)S(1)}, u32[]{:S(2)}, u32[]{:S(2)}) collective-permute-start(f32[3,2,24,384]{3,2,1,0:T(8,128)S(1)} %get-tuple-element.32), channel_id=1, source_target_pairs={{0,240},{16,0},{32,16},{48,32},{64,48},{80,64},{96,80},{112,96},{1... | collective-permute-start | bytes 663560 | tf_op jit(solution)/shard_map/ppermute | solution.py:25
  14.1 0.0 collective-permute-start.4
  14.1 0.0 collective-permute-done.1.across
  14.1 0.0 collective-permute-done.2.within
  14.2 3.6 %collective-permute-start.3 = (f32[3,2,3,4,384]{4,3,2,1,0:T(4,128)S(1)}, f32[3,2,3,4,384]{4,3,2,1,0:T(4,128)S(1)}, u32[]{:S(2)}, u32[]{:S(2)}) collective-permute-start(f32[3,2,3,4,384]{4,3,2,1,0:T(4,128)S(1)} %get-tuple-element.37), channel_id=1, source_target_pairs={{0,240},{16,0},{32,16},{48,32},{64,48},{80,64},{96,80},{112,96},{1... | collective-permute-start | bytes 331784 | tf_op jit(solution)/shard_map/ppermute | solution.py:25
  17.8 0.0 collective-permute-start.5
  17.8 0.8 %multiply_power_fusion = (f32[384]{0:T(512)S(1)}, f32[384]{0:T(512)S(1)}) fusion(f32[385]{0:T(512)} %param.3), kind=kLoop, calls=%fused_computation | loop fusion | flops 1152 | bytes 6144 | tf_op jit(solution)/shard_map/pow | solution.py:50
  18.7 0.0 copy-start.1
  18.7 1.3 %copy-done.1 = f32[3,8,32,384]{3,2,1,0:T(8,128)S(1)} copy-done((f32[3,8,32,384]{3,2,1,0:T(8,128)S(1)}, f32[3,8,32,384]{3,2,1,0:T(8,128)}, u32[]{:S(2)}) %copy-start.1) | copy-done | bytes 1179672
  20.0 3.9 %shard_map.59 = (f32[3,12,3,48,128]{4,3,2,1,0:T(8,128)S(1)}, f32[12,10,3,32,128]{4,3,2,1,0:T(8,128)S(1)}, f32[3,10,3,48,128]{4,3,2,1,0:T(8,128)S(1)}, f32[8,32,3...) custom-call(f32[3,8,2,384]{3,2,1,0:T(2,128)S(1)} %collective-permute-done, ...), custom_call_target="tpu_custom_call" | custom-call | flops 20000000 | tf_op jit(solution)/shard_map/pallas_call | solution.py:349
  23.8 1.5 %collective-permute-done.5.late = f32[3,2,3,4,384]{4,3,2,1,0:T(4,128)S(1)} collective-permute-done((f32[3,2,3,4,384]{4,3,2,1,0:T(4,128)S(1)}, f32[3,2,3,4,384]{4,3,2,1,0:T(4,128)S(1)}, u32[]{:S(2)}, u32[]{:S(2)}) %collective-permute-start.5) | collective-permute-done | bytes 110624 | tf_op jit(solution)/shard_map/ppermute | solution.py:25
  25.3 0.0 collective-permute-done.4.early
  25.3 1.4 %shard_map.60 = (f32[3,12,3,48,128]{4,3,2,1,0:T(8,128)S(1)}, f32[12,10,3,32,128]{4,3,2,1,0:T(8,128)S(1)}, f32[3,10,3,48,128]{4,3,2,1,0:T(8,128)S(1)}, f32[8,32,3...) custom-call(f32[3,2,24,384]{3,2,1,0:T(8,128)S(1)} %collective-permut, ...), custom_call_target="tpu_custom_call", output_to_operand_aliasing={{0}: (4, {}), {1}: (5, {}), {2}: (6, {}), {3}: (7, {}), {4}... | custom-call | flops 10000000 | tf_op jit(solution)/shard_map/pallas_call | solution.py:349
  26.7 0.0 collective-permute-done.3.late
  26.7 0.0 collective-permute-done.early
  26.7 1.5 %shard_map.61 = (f32[3,12,3,48,128]{4,3,2,1,0:T(8,128)S(1)}, f32[12,10,3,32,128]{4,3,2,1,0:T(8,128)S(1)}, f32[3,10,3,48,128]{4,3,2,1,0:T(8,128)S(1)}, f32[8,32,3...) custom-call(f32[3,2,24,384]{3,2,1,0:T(8,128)S(1)} %collective-permut, ...), custom_call_target="tpu_custom_call", output_to_operand_aliasing={{0}: (4, {}), {1}: (5, {}), {2}: (6, {}), {3}: (7, {}), {4}... | custom-call | flops 10000000 | tf_op jit(solution)/shard_map/pallas_call | solution.py:349
  28.2 13.8 %all_to_all.10 = f32[32,2,384]{2,1,0:T(2,128)S(1)} all-to-all(f32[32,2,384]{2,1,0:T(2,128)S(1)} %get-tuple-element.54), channel_id=1, replica_groups=mesh['gx_0'=8,'gx_1'=2,'gz_0'=4,'gz_1'=2,'gz_2'=2] {'gx_1','gz_0','gz_1'..., dimensions={0} | all-to-all | bytes 196608 | tf_op jit(solution)/shard_map/all_to_all | solution.py:44
  42.1 0.1 reduce_sum.9
  42.2 14.6 %all_to_all.11.parts_ref = f32[8,2,384]{2,1,0:T(2,128)S(1)} all-to-all(f32[8,2,384]{2,1,0:T(2,128)S(1)} %broadcast_in_dim.14), channel_id=1, replica_groups=mesh['gx_0'=8,'gx_1'=2,'gz_0'=4,'gz_1'=2,'gz_2'=2] {'gx_0'}, dimensions={0} | all-to-all | bytes 49152 | tf_op jit(solution)/shard_map/all_to_all | solution.py:46
  56.8 1.4 %finish.1 = (f32[8,32,384]{2,1,0:T(8,128)}, f32[8,32,384]{2,1,0:T(8,128)}, f32[8,32,384]{2,1,0:T(8,128)}, f32[384]{0:T(512)}) custom-call(f32[8,2,384]{2,1,0:T(2,128)S(1)} %all_to_all.11.parts_ref, f32[1,384]{1,0:T(1,128)S(1)} %broadcast_in_dim.13.width_ref, ...), custom_call_target="tpu_custom_call", output_to_operand_aliasing={{1}: (5, {}), {2}: (6, {})} | custom-call | tf_op jit(solution)/shard_map/finish/pallas_call | solution.py:421
  (4 shorter events, 0.1 us)
Async XLA Ops:
  0.6 1.3 %copy-start = (f32[3,8,32,384]{3,2,1,0:T(8,128)S(1)}, f32[3,8,32,384]{3,2,1,0:T(8,128)}, u32[]{:S(2)}) copy-start(f32[3,8,32,384]{3,2,1,0:T(8,128)} %v_ref.3) | copy-start | bytes 3538948
  2.0 12.1 %collective-permute-start.1 = (f32[3,8,2,384]{3,2,1,0:T(2,128)S(1)}, f32[3,8,2,384]{3,2,1,0:T(2,128)S(1)}, u32[]{:S(2)}, u32[]{:S(2)}) collective-permute-start(f32[3,8,2,384]{3,2,1,0:T(2,128)S(1)} %get-tuple-element.33), channel_id=1, source_target_pairs={{0,15},{1,2},{2,1},{3,4},{4,3},{5,6},{6,5},{7,8},{8,7},{9,10},{10,... | collective-permute-start | bytes 221192 | tf_op jit(solution)/shard_map/ppermute | solution.py:25
  6.2 7.9 %collective-permute-start.2 = (f32[3,8,2,384]{3,2,1,0:T(2,128)S(1)}, f32[3,8,2,384]{3,2,1,0:T(2,128)S(1)}, u32[]{:S(2)}, u32[]{:S(2)}) collective-permute-start(f32[3,8,2,384]{3,2,1,0:T(2,128)S(1)} %get-tuple-element.34), channel_id=1, source_target_pairs={{0,1},{1,0},{2,3},{3,2},{4,5},{5,4},{6,7},{7,6},{8,9},{9,8},{10,11... | collective-permute-start | bytes 221192 | tf_op jit(solution)/shard_map/ppermute | solution.py:25
  8.5 18.2 %collective-permute-start = (f32[3,2,24,384]{3,2,1,0:T(8,128)S(1)}, f32[3,2,24,384]{3,2,1,0:T(8,128)S(1)}, u32[]{:S(2)}, u32[]{:S(2)}) collective-permute-start(f32[3,2,24,384]{3,2,1,0:T(8,128)S(1)} %get-tuple-element.32), channel_id=1, source_target_pairs={{0,240},{16,0},{32,16},{48,32},{64,48},{80,64},{96,80},{112,96},{1... | collective-permute-start | bytes 663560 | tf_op jit(solution)/shard_map/ppermute | solution.py:25
  14.1 11.2 %collective-permute-start.4 = (f32[3,2,24,384]{3,2,1,0:T(8,128)S(1)}, f32[3,2,24,384]{3,2,1,0:T(8,128)S(1)}, u32[]{:S(2)}, u32[]{:S(2)}) collective-permute-start(f32[3,2,24,384]{3,2,1,0:T(8,128)S(1)} %get-tuple-element.38), channel_id=1, source_target_pairs={{0,16},{16,32},{32,48},{48,64},{64,80},{80,96},{96,112},{112,128},... | collective-permute-start | bytes 663560 | tf_op jit(solution)/shard_map/ppermute | solution.py:25
  14.2 12.6 %collective-permute-start.3 = (f32[3,2,3,4,384]{4,3,2,1,0:T(4,128)S(1)}, f32[3,2,3,4,384]{4,3,2,1,0:T(4,128)S(1)}, u32[]{:S(2)}, u32[]{:S(2)}) collective-permute-start(f32[3,2,3,4,384]{4,3,2,1,0:T(4,128)S(1)} %get-tuple-element.37), channel_id=1, source_target_pairs={{0,240},{16,0},{32,16},{48,32},{64,48},{80,64},{96,80},{112,96},{1... | collective-permute-start | bytes 331784 | tf_op jit(solution)/shard_map/ppermute | solution.py:25
  17.8 7.5 %collective-permute-start.5 = (f32[3,2,3,4,384]{4,3,2,1,0:T(4,128)S(1)}, f32[3,2,3,4,384]{4,3,2,1,0:T(4,128)S(1)}, u32[]{:S(2)}, u32[]{:S(2)}) collective-permute-start(f32[3,2,3,4,384]{4,3,2,1,0:T(4,128)S(1)} %get-tuple-element.39), channel_id=1, source_target_pairs={{0,16},{16,32},{32,48},{48,64},{64,80},{80,96},{96,112},{112,128},... | collective-permute-start | bytes 331784 | tf_op jit(solution)/shard_map/ppermute | solution.py:25
  18.7 1.3 %copy-start.1 = (f32[3,8,32,384]{3,2,1,0:T(8,128)S(1)}, f32[3,8,32,384]{3,2,1,0:T(8,128)}, u32[]{:S(2)}) copy-start(f32[3,8,32,384]{3,2,1,0:T(8,128)} %v_ref.3) | copy-start | bytes 3538948
